TPU v7x, 32 devices: a whole 2x2x4 slice. The times are simulated.
32 devices in a mesh: group: 2 (over y), hi: 4 (over z), lo: 2 (over x), cuts: 2 (over core).
Axes of the slice: x: 2, y: 2, z: 4, core: 2. Of those that a mesh axis runs over, the one named last changes fastest.
Arguments:
- state_block: float32 [8, 2, 131072], P(('group', 'hi'), 'lo'), parts along dimension 0, may hold values from -6 to 6
- gate_table: float32 [4, 256, 256], replicated, may hold values from -0.375 to 0.375
- closing_table: float32 [4, 2, 2, 256], replicated, may hold values from -1 to 1
- slice_edges: int32 [8, 3], P(('group', 'cuts')), parts along dimension 0, may hold values from 0 to 3
- bit_orders: int32 [2, 8], replicated, may hold values from 0 to 7, each once within a row
Outputs:
- amplitudes: float32 [8, 2, 65536], P(('group', 'hi'), 'lo', 'cuts'), parts along dimension 0
There are 2 independent parts, one for each index of `group`. A program takes and returns all parts, laid end to end along the dimension named above; an argument that names none is the same for every part. Nothing has to cross between parts.
Inputs may be any that keep to these rules, and one draw needn't show every extreme that they name: `bit_orders`: each row is a permutation of 0 to 7.
All inputs are finite; a program needn't handle non-finite values.
Results may differ from a plain program's by a relative error of at most 0.0001.
Values sent between devices are 32-bit elements; how exact they have to be, the bound alone decides.
A program may use at most 64 MiB of HBM per device.

v0:
```python
import jax
import jax.numpy as jnp
from jax import lax
from jax.sharding import PartitionSpec as P

BITS = 8
GATE = 256
CLOSED = 2


def permuted(gate, order):
    rows = jnp.arange(GATE, dtype=jnp.int32)
    picked = rows[:, None] >> order[None, :] & 1
    weights = jnp.left_shift(jnp.ones((BITS,), jnp.int32), jnp.arange(BITS, dtype=jnp.int32))
    source = jnp.sum(picked * weights[None, :], axis=1)
    return jnp.take(gate, source, axis=0)


def local(state_block, gate_table, closing_table, slice_edges, bit_orders):
    count_hi = lax.axis_size("hi")
    count_lo = lax.axis_size("lo")
    span_hi = GATE // count_hi
    span_lo = GATE // count_lo
    middle = state_block.shape[2] // (GATE * GATE * CLOSED)
    tensor = state_block.reshape(span_hi, count_hi, CLOSED, middle, count_lo, span_lo)
    turns = slice_edges.shape[0]
    firsts = []
    seconds = []
    fronts = []
    rears = []
    for turn_index in range(turns):
        chosen = slice_edges[turn_index]
        firsts.append(permuted(gate_table[chosen[0]], bit_orders[0]))
        seconds.append(permuted(gate_table[chosen[1]], bit_orders[1]))
        fronts.append(closing_table[chosen[2], 0])
        rears.append(closing_table[chosen[2], 1])
    section_ones = []
    for turn_index in range(turns):

        def apply_first(piece, first=firsts[turn_index], front=fronts[turn_index]):
            shape = piece.shape
            flat = piece.reshape(GATE, -1)
            product = lax.dot_general(
                first,
                flat,
                (((0,), (0,)), ((), ())),
                precision=lax.Precision.HIGHEST,
                preferred_element_type=jnp.float32,
            )
            scaled = jnp.transpose(front).reshape(shape[0], shape[1], shape[2], 1, 1, 1)
            return product.reshape(shape) * scaled

        section_ones.append(
            apply_first(lax.all_to_all(tensor, "hi", split_axis=1, concat_axis=1, tiled=True))
        )
    total = jnp.zeros((span_hi, count_hi, middle, count_lo, span_lo), jnp.float32)
    for turn_index in range(turns):
        current = section_ones[turn_index]

        def apply_second(piece, second=seconds[turn_index], rear=rears[turn_index]):
            shape = piece.shape
            flat = piece.reshape(-1, GATE)
            product = jnp.dot(
                flat, second, precision=lax.Precision.HIGHEST, preferred_element_type=jnp.float32
            )
            product = product.reshape(shape[0], shape[1], shape[2], shape[3], GATE)
            closed = jnp.einsum("phzkg,zg->phkg", product, rear, precision=lax.Precision.HIGHEST)
            return closed.reshape(shape[0], shape[1], shape[3], shape[4], shape[5])

        total = total + apply_second(
            lax.all_to_all(current, "lo", split_axis=4, concat_axis=4, tiled=True)
        )
    placed = lax.all_to_all(
        lax.all_to_all(total, "hi", split_axis=1, concat_axis=1, tiled=True),
        "lo",
        split_axis=3,
        concat_axis=3,
        tiled=True,
    )
    summed = lax.psum_scatter(placed.reshape(-1), "cuts", scatter_dimension=0, tiled=True)
    return summed.reshape(1, 1, -1)


def solution(mesh):
    in_specs = (P(("group", "hi"), "lo", None), P(), P(), P(("group", "cuts"), None), P())
    out_specs = P(("group", "hi"), "lo", "cuts")
    return jax.shard_map(local, mesh=mesh, in_specs=in_specs, out_specs=out_specs, check_vma=False)
```

profile of v0, /device:TPU:0, one launch (start us, length us, event | category | flops | bytes accessed | tf_op | source)
XLA Modules:
  0.0 101.6 jit_solution(624355005231867569)
XLA Ops:
  6.5 0.0 copy-start
  6.5 2.1 %copy.48 = f32[64,4,2,1,2,128]{5,4,2,0,3,1:T(2,128)} copy(f32[64,4,2,1,2,128]{5,4,2,1,0,3:T(2,128)} %bitcast.102) | data formatting | bytes 1048576 | tf_op jit(solution)/shard_map/reshape | solution.py:25
  8.6 0.0 copy-start.1
  8.6 6.5 %all-to-all-start = ((f32[64,4,2,1,2,128]{5,4,2,0,3,1:T(2,128)}), f32[64,4,2,1,2,128]{5,4,2,0,3,1:T(2,128)S(1)}, u32[]{:S(2)}, u32[]{:S(2)}) async-start(f32[64,4,2,1,2,128]{5,4,2,0,3,1:T(2,128)} %copy.48), calls=%async_computation | async-start | bytes 1048576 | tf_op jit(solution)/shard_map/all_to_all | solution.py:54
  15.1 0.0 copy-done.1
  15.1 0.6 fusion.18
  22.5 0.0 copy-start.3
  23.1 0.1 copy-done.3
  25.7 0.1 multiply_reduce_fusion
  25.8 0.0 copy-done
  25.8 0.1 dynamic-slice_bitcast_fusion
  25.9 1.0 gather_fusion
  26.9 1.0 gather_fusion.2
  27.9 0.1 select_bitcast_fusion
  28.0 0.1 copy.55
  28.1 0.0 copy-start.2
  28.1 0.1 dot_general.43
  29.4 0.0 copy-done.2
  29.4 0.1 mul.57
  29.6 0.1 copy.57
  29.6 0.0 all-to-all-done
  29.6 0.2 copy.49
  29.8 0.4 reshape.99
  30.3 0.2 copy.50
  30.5 0.6 fusion.2
  31.1 0.8 copy.58
  31.9 3.5 %all-to-all-start.2 = ((f32[64,4,2,1,2,128]{5,0,2,1,3,4:T(8,128)}), f32[64,4,2,1,2,128]{5,0,2,1,3,4:T(8,128)S(1)}, u32[]{:S(2)}, u32[]{:S(2)}) async-start(f32[64,4,2,1,2,128]{5,0,2,1,3,4:T(8,128)} %copy.58), calls=%async_computation.2 | async-start | bytes 1048576 | tf_op jit(solution)/shard_map/all_to_all | solution.py:71
  35.4 0.1 copy.47
  35.6 0.1 dot_general.35
  35.7 0.1 mul.52
  35.8 0.1 copy.52
  35.9 0.6 fusion.3
  36.5 0.8 copy.53
  37.3 6.1 %all-to-all-done.2 = f32[64,4,2,1,2,128]{5,0,2,1,3,4:T(8,128)S(1)} async-done(((f32[64,4,2,1,2,128]{5,0,2,1,3,4:T(8,128)}), f32[64,4,2,1,2,128]{5,0,2,1,3,4:T(8,128)S(1)}, u32[]{:S(2)}, u32[]{:S(2)}) %all-to-all-start.2) | async-done | bytes 524320 | tf_op jit(solution)/shard_map/all_to_all | solution.py:71
  43.4 3.5 %all-to-all-start.1 = ((f32[64,4,2,1,2,128]{5,0,2,1,3,4:T(8,128)}), f32[64,4,2,1,2,128]{5,0,2,1,3,4:T(8,128)S(1)}, u32[]{:S(2)}, u32[]{:S(2)}) async-start(f32[64,4,2,1,2,128]{5,0,2,1,3,4:T(8,128)} %copy.53), calls=%async_computation.1 | async-start | bytes 1048576 | tf_op jit(solution)/shard_map/all_to_all | solution.py:71
  46.9 0.0 all-reduce.3.cloned.1.call-start
  47.0 1.0 gather_fusion.3
  47.9 1.0 gather_fusion.1
  48.9 0.4 copy.59
  49.3 0.4 dot_general.45
  49.8 4.2 %all-to-all-done.1 = f32[64,4,2,1,2,128]{5,0,2,1,3,4:T(8,128)S(1)} async-done(((f32[64,4,2,1,2,128]{5,0,2,1,3,4:T(8,128)}), f32[64,4,2,1,2,128]{5,0,2,1,3,4:T(8,128)S(1)}, u32[]{:S(2)}, u32[]{:S(2)}) %all-to-all-start.1) | async-done | bytes 524320 | tf_op jit(solution)/shard_map/all_to_all | solution.py:71
  54.0 0.4 copy.54
  54.4 0.4 dot_general.39
  54.8 0.7 fusion.4
  55.5 0.7 fusion.5
  56.2 0.1 add.57
  56.4 11.5 %all_to_all.26 = f32[64,4,1,2,128]{4,3,0,2,1:T(2,128)S(1)} all-to-all(f32[64,4,1,2,128]{4,3,0,2,1:T(2,128)S(1)} %add.57), channel_id=1, replica_groups=mesh['group'=2,'hi'=4,'lo'=2,'cuts'=2] {'hi'}, dimensions={1} | all-to-all | bytes 524288 | tf_op jit(solution)/shard_map/all_to_all | solution.py:74
  67.8 0.2 copy.60
  68.0 7.6 %all_to_all.27 = f32[64,4,1,2,128]{4,1,0,2,3:T(4,128)S(1)} all-to-all(f32[64,4,1,2,128]{4,1,0,2,3:T(4,128)S(1)} %copy.60), channel_id=1, replica_groups=mesh['group'=2,'hi'=4,'lo'=2,'cuts'=2] {'lo'}, dimensions={3} | all-to-all | bytes 524288 | tf_op jit(solution)/shard_map/all_to_all | solution.py:73
  75.6 0.9 copy.61
  76.5 0.0 all-reduce.3.cloned.1.call-update
  76.5 0.0 copy-start.4
  76.5 0.6 copy-done.4
  77.2 0.6 dynamic-slice
  78.4 14.8 %all-reduce.3.cloned.1.call-done = f32[65536]{0:T(1024)} async-done(((f32[65536]{0:T(1024)}), f32[65536]{0:T(1024)}) %all-reduce.3.cloned.1.call-update) | async-done | bytes 262160
  93.2 1.6 %dynamic-slice.1 = f32[32768]{0:T(1024)} dynamic-slice(f32[65536]{0:T(1024)} %all-reduce.3.cloned.1.call-done, u32[]{:T(128)S(6)} %multiply.3), dynamic_slice_sizes={32768} | dynamic-slice | bytes 262148
  (9 shorter events, 0.1 us)
Async XLA Ops:
  6.5 19.3 %copy-start = (f32[4,256,256]{2,1,0:T(8,128)S(1)}, f32[4,256,256]{2,1,0:T(8,128)}, u32[]{:S(2)}) copy-start(f32[4,256,256]{2,1,0:T(8,128)} %param.8) | copy-start | bytes 3145732
  8.6 6.5 %copy-start.1 = (s32[2,3]{1,0:T(2,128)S(1)}, s32[2,3]{1,0:T(2,128)}, u32[]{:S(2)}) copy-start(s32[2,3]{1,0:T(2,128)} %param.10) | copy-start | bytes 76
  8.6 21.0 %all-to-all-start = ((f32[64,4,2,1,2,128]{5,4,2,0,3,1:T(2,128)}), f32[64,4,2,1,2,128]{5,4,2,0,3,1:T(2,128)S(1)}, u32[]{:S(2)}, u32[]{:S(2)}) async-start(f32[64,4,2,1,2,128]{5,4,2,0,3,1:T(2,128)} %copy.48), calls=%async_computation | async-start | bytes 1048576 | tf_op jit(solution)/shard_map/all_to_all | solution.py:54
  22.5 0.7 copy-start.3
  28.1 1.3 %copy-start.2 = (f32[4,2,2,256]{3,2,1,0:T(2,128)S(1)}, f32[4,2,2,256]{3,2,1,0:T(2,128)}, u32[]{:S(2)}) copy-start(f32[4,2,2,256]{3,2,1,0:T(2,128)} %param.9) | copy-start | bytes 49156
  31.9 11.5 %all-to-all-start.2 = ((f32[64,4,2,1,2,128]{5,0,2,1,3,4:T(8,128)}), f32[64,4,2,1,2,128]{5,0,2,1,3,4:T(8,128)S(1)}, u32[]{:S(2)}, u32[]{:S(2)}) async-start(f32[64,4,2,1,2,128]{5,0,2,1,3,4:T(8,128)} %copy.58), calls=%async_computation.2 | async-start | bytes 1048576 | tf_op jit(solution)/shard_map/all_to_all | solution.py:71
  43.4 10.6 %all-to-all-start.1 = ((f32[64,4,2,1,2,128]{5,0,2,1,3,4:T(8,128)}), f32[64,4,2,1,2,128]{5,0,2,1,3,4:T(8,128)S(1)}, u32[]{:S(2)}, u32[]{:S(2)}) async-start(f32[64,4,2,1,2,128]{5,0,2,1,3,4:T(8,128)} %copy.53), calls=%async_computation.1 | async-start | bytes 1048576 | tf_op jit(solution)/shard_map/all_to_all | solution.py:71
  46.9 46.3 %all-reduce.3.cloned.1.call-start = ((), (), s32[]{:S(2)}) async-start(), calls=%async_computation.5 | async-start | bytes 524288
  76.5 0.7 copy-start.4
Sparse Core Ops, SparseCore 0:
  76.6 16.5 all-reduce.2
where the time goes:
time: 102 us
  between operations  25.4 us (25%)
  waiting for transfers between devices  25.1 us (25%)
  blocking collectives  19 us (19%)
  local copies, waits for them, and re-layouts  15.7 us (15%)
  starting transfers between devices  13.5 us (13%)
  matrix products  2.62 us (3%)
    unnamed x2, waiting for transfers between devices  14.8 us
    all_to_all x1, blocking collectives, local(): lax.all_to_all(total, 'hi', split_axis=1, concat_axis=1, tiled=True)  11.5 us
    all_to_all x2, waiting for transfers between devices, local(): lax.all_to_all(current, 'lo', split_axis=4, concat_axis=4, tiled=True)  10.3 us
    all_to_all x1, blocking collectives, local(): lax.all_to_all(lax.all_to_all(total, 'hi', split_axis=1, concat_axis=1, t...  7.56 us
    all_to_all x2, starting transfers between devices, local(): lax.all_to_all(current, 'lo', split_axis=4, concat_axis=4, tiled=True)  6.97 us
    all_to_all x1, starting transfers between devices, local(): lax.all_to_all(tensor, 'hi', split_axis=1, concat_axis=1, tiled=True)  6.48 us
    gather x4, local copies, waits for them, and re-layouts, permuted(): return jnp.take(gate, source, axis=0)  3.88 us
    unnamed x13, local copies, waits for them, and re-layouts  2.92 us
  transfers between devices with their start and end apart: 4, of which 3 were waited for; matrix products, arithmetic and copies ran while one was open for 8% of the time, Pallas kernels for 0%

commit v1 on v0

--- a/solution.py
+++ b/solution.py
@@ -1,6 +1,10 @@
+import functools
+
 import jax
 import jax.numpy as jnp
 from jax import lax
+from jax.experimental import pallas as pl
+from jax.experimental.pallas import tpu as pltpu
 from jax.sharding import PartitionSpec as P
 
 BITS = 8
@@ -16,7 +20,7 @@
     return jnp.take(gate, source, axis=0)
 
 
-def local(state_block, gate_table, closing_table, slice_edges, bit_orders):
+def local_plain(state_block, gate_table, closing_table, slice_edges, bit_orders):
     count_hi = lax.axis_size("hi")
     count_lo = lax.axis_size("lo")
     span_hi = GATE // count_hi
@@ -81,6 +85,275 @@
     return summed.reshape(1, 1, -1)
 
 
+MESH = pl.DeviceIdType.MESH
+HALF = jnp.bfloat16
+FULL = jnp.float32
+
+
+def dot(left, right, dims=((1,), (0,))):
+    return lax.dot_general(left, right, (dims, ((), ())), preferred_element_type=FULL)
+
+
+def halves(value):
+    high = value.astype(HALF)
+    return high, (value - high.astype(FULL)).astype(HALF)
+
+
+def source_row(index, orders_ref, section):
+    total = jnp.zeros_like(index)
+    for bit in range(BITS):
+        picked = lax.shift_right_logical(index, jnp.full_like(index, orders_ref[section, bit])) & 1
+        total = total | (picked << bit)
+    return total
+
+
+def kernel(
+    count_hi,
+    count_lo,
+    x_hbm,
+    gate_hbm,
+    closing_hbm,
+    edges_hbm,
+    orders_hbm,
+    out_ref,
+    x_ref,
+    gate_ref,
+    closing_ref,
+    edges_ref,
+    orders_ref,
+    outgoing,
+    arrived,
+    edges_far,
+    first_ref,
+    second_ref,
+    part_near,
+    part_far,
+    result,
+    landed,
+    local_sems,
+    edge_sems,
+    part_sems,
+    in_send,
+    in_recv,
+    out_send,
+    out_recv,
+):
+    hi, lo, cut = lax.axis_index("hi"), lax.axis_index("lo"), lax.axis_index("cuts")
+    other = 1 - cut
+    span_hi, span_lo = GATE // count_hi, GATE // count_lo
+    rows = GATE // 2
+    turns = edges_ref.shape[0]
+    edges = gate_ref.shape[0]
+    offsets = [
+        (a, b) for a in range(count_hi - 1, -1, -1) for b in range(count_lo) if a or b
+    ]
+    pairs = (
+        (x_hbm, x_ref),
+        (edges_hbm, edges_ref),
+        (orders_hbm, orders_ref),
+        (closing_hbm, closing_ref),
+        (gate_hbm, gate_ref),
+    )
+    gets = [pltpu.make_async_copy(*pair, local_sems.at[i]) for i, pair in enumerate(pairs)]
+    for get in gets:
+        get.start()
+
+    def target(a, b):
+        return lax.rem(hi + a, count_hi), lax.rem(lo + b, count_lo)
+
+    barrier = pltpu.get_barrier_semaphore()
+    for a, b in offsets:
+        th, tl = target(a, b)
+        pl.semaphore_signal(barrier, inc=1, device_id={"hi": th, "lo": tl}, device_id_type=MESH)
+    pl.semaphore_signal(barrier, inc=1, device_id={"cuts": other}, device_id_type=MESH)
+
+    gets[0].wait()
+    stride = count_hi * CLOSED * count_lo
+    for b in range(count_hi):
+        for e in range(count_lo):
+            start = b * CLOSED * count_lo + cut * count_lo + e
+            outgoing[b * count_lo + e] = x_ref[pl.ds(start, span_hi, stride=stride), :]
+    arrived[lo, pl.ds(pl.multiple_of(hi * span_hi, span_hi), span_hi), :] = outgoing[
+        hi * count_lo + lo
+    ]
+    pl.semaphore_wait(barrier, len(offsets) + 1)
+
+    sends = []
+    for k, (a, b) in enumerate(offsets):
+        th, tl = target(a, b)
+        copy = pltpu.make_async_remote_copy(
+            src_ref=outgoing.at[th * count_lo + tl],
+            dst_ref=arrived.at[lo, pl.ds(pl.multiple_of(hi * span_hi, span_hi), span_hi), :],
+            send_sem=in_send.at[k],
+            recv_sem=in_recv.at[k],
+            device_id={"hi": th, "lo": tl},
+            device_id_type=MESH,
+        )
+        copy.start()
+        sends.append(copy)
+    gets[1].wait()
+    edge_copy = pltpu.make_async_remote_copy(
+        src_ref=edges_ref,
+        dst_ref=edges_far,
+        send_sem=edge_sems.at[0],
+        recv_sem=edge_sems.at[1],
+        device_id={"cuts": other},
+        device_id_type=MESH,
+    )
+    edge_copy.start()
+
+    gets[2].wait()
+    down = lax.broadcasted_iota(jnp.int32, (GATE, GATE), 0)
+    along = lax.broadcasted_iota(jnp.int32, (GATE, GATE), 1)
+    per = span_hi // 2
+    column = (down // rows * per + down % per) * count_hi + down % rows // per
+    columns = (column == along).astype(FULL).astype(HALF)
+    rows_one = source_row(along % span_hi * count_hi + along // span_hi, orders_ref, 0)
+    rows_one = (rows_one == down).astype(FULL).astype(HALF)
+    rows_two = (source_row(down, orders_ref, 1) == along).astype(FULL).astype(HALF)
+
+    gets[3].wait()
+    gets[4].wait()
+    edge_copy.wait()
+    for s in range(2 * turns):
+        chosen = edges_ref if s < turns else edges_far
+        turn = s % turns
+
+        def pick(place, values):
+            total = None
+            for c in range(edges):
+                weight = (chosen[turn : turn + 1, place : place + 1] == c).astype(FULL)
+                term = weight * values(c)
+                total = term if total is None else total + term
+            return total
+
+        front = pick(2, lambda c: closing_ref[c, 0, pl.ds(cut, 1), :])
+        rear = pick(2, lambda c: closing_ref[c, 1, pl.ds(cut, 1), :])
+        for part, piece in enumerate(halves(pick(0, lambda c: gate_ref[c]) * front)):
+            moved = dot(columns, piece, ((1,), (1,))).astype(HALF)
+            moved = dot(moved, rows_one).astype(HALF)
+            for side in range(2):
+                first_ref[part, side, pl.ds(s * rows, rows), :] = moved[
+                    side * rows : (side + 1) * rows
+                ]
+        for part, piece in enumerate(halves(pick(1, lambda c: gate_ref[c]) * rear)):
+            second_ref[part, pl.ds(s * GATE, GATE), :] = dot(rows_two, piece).astype(HALF)
+
+    for copy in sends:
+        copy.wait_recv()
+    x_high, x_low = halves(jnp.concatenate([arrived[i] for i in range(count_lo)], axis=1))
+
+    def amplitudes(side):
+        high, low = first_ref[0, side], first_ref[1, side]
+        inner = dot(high, x_high) + dot(high, x_low) + dot(low, x_high)
+        inner_high, inner_low = halves(inner)
+        total = None
+        for s in range(2 * turns):
+            left_high = inner_high[s * rows : (s + 1) * rows]
+            left_low = inner_low[s * rows : (s + 1) * rows]
+            right_high = second_ref[0, pl.ds(s * GATE, GATE), :]
+            right_low = second_ref[1, pl.ds(s * GATE, GATE), :]
+            term = dot(left_high, right_high) + dot(left_high, right_low) + dot(left_low, right_high)
+            total = term if total is None else total + term
+        return total
+
+    part_near[...] = amplitudes(other)
+    part_copy = pltpu.make_async_remote_copy(
+        src_ref=part_near,
+        dst_ref=part_far,
+        send_sem=part_sems.at[0],
+        recv_sem=part_sems.at[1],
+        device_id={"cuts": other},
+        device_id_type=MESH,
+    )
+    part_copy.start()
+    own = amplitudes(cut)
+    part_copy.wait_recv()
+    own = own + part_far[...]
+    for b in range(count_hi):
+        for e in range(count_lo):
+            result[b * count_lo + e] = own[b * per : (b + 1) * per, e * span_lo : (e + 1) * span_lo]
+    here = hi * count_lo + lo
+    outs = []
+    for k, (a, b) in enumerate(offsets):
+        th, tl = target(a, b)
+        copy = pltpu.make_async_remote_copy(
+            src_ref=result.at[th * count_lo + tl],
+            dst_ref=landed.at[here],
+            send_sem=out_send.at[k],
+            recv_sem=out_recv.at[k],
+            device_id={"hi": th, "lo": tl},
+            device_id_type=MESH,
+        )
+        copy.start()
+        outs.append(copy)
+    landed[here] = result[here]
+    for copy in outs:
+        copy.wait_recv()
+    for j in range(count_hi * count_lo):
+        out_ref[pl.ds(j, per, stride=count_hi * count_lo), :] = landed[j]
+    for copy in sends:
+        copy.wait_send()
+    part_copy.wait_send()
+    for copy in outs:
+        copy.wait_send()
+
+
+def local(state_block, gate_table, closing_table, slice_edges, bit_orders):
+    count_hi = lax.axis_size("hi")
+    count_lo = lax.axis_size("lo")
+    span_hi = GATE // count_hi
+    span_lo = GATE // count_lo
+    blocks = count_hi * count_lo
+    middle = state_block.shape[2] // (GATE * GATE * CLOSED)
+    fits = middle == 1 and span_lo == 128 and span_hi % 16 == 0
+    if not fits or lax.axis_size("cuts") != CLOSED:
+        return local_plain(state_block, gate_table, closing_table, slice_edges, bit_orders)
+    slices = slice_edges.shape[0] * CLOSED
+    rows = GATE // 2
+    hbm = pl.BlockSpec(memory_space=pltpu.HBM)
+    dma = pltpu.SemaphoreType.DMA
+    out = pl.pallas_call(
+        functools.partial(kernel, count_hi, count_lo),
+        out_shape=jax.ShapeDtypeStruct((span_hi // 2 * blocks, span_lo), FULL),
+        in_specs=[hbm] * 5,
+        out_specs=pl.BlockSpec(memory_space=pltpu.VMEM),
+        scratch_shapes=[
+            pltpu.VMEM((span_hi * blocks * CLOSED, span_lo), FULL),
+            pltpu.VMEM(gate_table.shape, FULL),
+            pltpu.VMEM(closing_table.shape, FULL),
+            pltpu.VMEM(slice_edges.shape, jnp.int32),
+            pltpu.SMEM(bit_orders.shape, jnp.int32),
+            pltpu.VMEM((blocks, span_hi, span_lo), FULL),
+            pltpu.VMEM((count_lo, GATE, span_lo), FULL),
+            pltpu.VMEM(slice_edges.shape, jnp.int32),
+            pltpu.VMEM((2, 2, slices * rows, GATE), HALF),
+            pltpu.VMEM((2, slices * GATE, GATE), HALF),
+            pltpu.VMEM((rows, GATE), FULL),
+            pltpu.VMEM((rows, GATE), FULL),
+            pltpu.VMEM((blocks, span_hi // 2, span_lo), FULL),
+            pltpu.VMEM((blocks, span_hi // 2, span_lo), FULL),
+            dma((5,)),
+            dma((2,)),
+            dma((2,)),
+            dma((blocks,)),
+            dma((blocks,)),
+            dma((blocks,)),
+            dma((blocks,)),
+        ],
+        compiler_params=pltpu.CompilerParams(
+            collective_id=0, has_side_effects=True, vmem_limit_bytes=32 * 1024 * 1024
+        ),
+    )(
+        state_block.reshape(-1, span_lo),
+        gate_table,
+        closing_table,
+        slice_edges,
+        bit_orders,
+    )
+    return out.reshape(1, 1, -1)
+
+
 def solution(mesh):
     in_specs = (P(("group", "hi"), "lo", None), P(), P(), P(("group", "cuts"), None), P())
     out_specs = P(("group", "hi"), "lo", "cuts")

time: 102 us -> 26.8 us (0.26)
  between operations: 25.4 us -> 0.01 us
  waiting for transfers between devices: 25.1 us -> 0 us
  Pallas kernels: 0 us -> 21.5 us
  blocking collectives: 19 us -> 0 us
  starting transfers between devices: 13.5 us -> 0 us
  local copies, waits for them, and re-layouts: 15.7 us -> 5 us
  matrix products: 2.62 us -> 0 us
    pallas_call x0 -> x1, Pallas kernels: none -> 21.5 us  [local(): pl.pallas_call(functools.partial(kernel, count_hi, count_lo), out_shape=j...]
    all_to_all x2 -> x0, blocking collectives: 19 us -> none  [the longest x1 11.5 us: local(): lax.all_to_all(total, 'hi', split_axis=1, concat_axis=1, tiled=True)]
    unnamed x2 -> x0, waiting for transfers between devices: 14.8 us -> none
    all_to_all x3 -> x0, starting transfers between devices: 13.5 us -> none  [the longest x2 6.97 us: local(): lax.all_to_all(current, 'lo', split_axis=4, concat_axis=4, tiled=True)]
    all_to_all x3 -> x0, waiting for transfers between devices: 10.3 us -> none  [the longest x2 10.3 us: local(): lax.all_to_all(current, 'lo', split_axis=4, concat_axis=4, tiled=True)]
    gather x4 -> x0, local copies, waits for them, and re-layouts: 3.88 us -> none  [permuted(): return jnp.take(gate, source, axis=0)]
    dot_general x4 -> x0, matrix products: 2.62 us -> none  [the longest x2 1.33 us: apply_second(): jnp.dot(flat, second, precision=lax.Precision.HIGHEST, preferred_element_...]
    reshape x2 -> x0, local copies, waits for them, and re-layouts: 2.52 us -> none  [the longest x1 2.1 us: local(): state_block.reshape(span_hi, count_hi, CLOSED, middle, count_lo, span_lo)]
  transfers between devices with their start and end apart: 4 -> 0, of which waited for: 3 -> 0; matrix products, arithmetic and copies ran while one was open for 8% -> 0% of each run, Pallas kernels for 0% -> 0%
where the time goes in v1:
time: 26.8 us; the launch traced here: 26.5 us
  Pallas kernels  21.5 us (80%)
  local copies, waits for them, and re-layouts  5 us (19%)
    pallas_call x1, Pallas kernels, local(): pl.pallas_call(functools.partial(kernel, count_hi, count_lo), out_shape=j...  21.5 us
    unnamed x11, local copies, waits for them, and re-layouts  5 us

profile of v1, /device:TPU:0, one launch (start us, length us, event | category | flops | bytes accessed | tf_op | source)
XLA Modules:
  0.0 26.5 jit_solution(861878740662676383)
XLA Ops:
  0.0 0.0 copy-start.3
  0.0 0.7 %copy-done.3 = s32[2,3]{1,0:T(2,128)S(1)} copy-done((s32[2,3]{1,0:T(2,128)S(1)}, s32[2,3]{1,0:T(2,128)}, u32[]{:S(2)}) %copy-start.3) | copy-done | bytes 48
  0.7 0.0 copy-start
  0.7 1.2 %copy-done = f32[4,256,256]{2,1,0:T(8,128)S(1)} copy-done((f32[4,256,256]{2,1,0:T(8,128)S(1)}, f32[4,256,256]{2,1,0:T(8,128)}, u32[]{:S(2)}) %copy-start) | copy-done | bytes 1048600
  1.9 0.0 copy-start.1
  1.9 1.0 %copy-done.1 = f32[1,1,131072]{2,1,0:T(1,128)S(1)} copy-done((f32[1,1,131072]{2,1,0:T(1,128)S(1)}, f32[1,1,131072]{2,1,0:T(1,128)}, u32[]{:S(2)}) %copy-start.1) | copy-done | bytes 524312
  2.9 0.0 copy-start.2
  2.9 0.7 %copy-done.2 = f32[4,2,2,256]{3,2,1,0:T(2,128)S(1)} copy-done((f32[4,2,2,256]{3,2,1,0:T(2,128)S(1)}, f32[4,2,2,256]{3,2,1,0:T(2,128)}, u32[]{:S(2)}) %copy-start.2) | copy-done | bytes 16408
  3.7 0.0 copy-start.4
  3.7 0.7 %copy-done.4 = s32[2,8]{1,0:T(2,128)S(1)} copy-done((s32[2,8]{1,0:T(2,128)S(1)}, s32[2,8]{1,0:T(2,128)}, u32[]{:S(2)}) %copy-start.4) | copy-done | bytes 88
  4.3 21.5 %shard_map.55 = f32[256,128]{1,0:T(8,128)S(1)} custom-call(f32[1024,128]{1,0:T(8,128)S(1)} %bitcast.2, f32[4,256,256]{2,1,0:T(8,128)S(1)} %copy-done, f32[4,2,2,256]{3,2,1,0:T(2,128)S(1)} %copy-done.2, s32[2,3]{1,0:T(2,128)S(1)} %copy-done.3, s32[2,8]{1,0:T(2,128)S(1)} %copy-done.4), custom_call_target="tpu_custom_call" | custom-call | tf_op jit(solution)/shard_map/pallas_call | solution.py:316
  25.8 0.7 %copy.7 = f32[1,1,32768]{2,1,0:T(1,128)} copy(f32[1,1,32768]{2,1,0:T(1,128)S(1)} %bitcast.3) | data formatting | bytes 262144
Async XLA Ops:
  0.0 0.7 %copy-start.3 = (s32[2,3]{1,0:T(2,128)S(1)}, s32[2,3]{1,0:T(2,128)}, u32[]{:S(2)}) copy-start(s32[2,3]{1,0:T(2,128)} %edges_hbm.1) | copy-start | bytes 76
  0.7 1.2 %copy-start = (f32[4,256,256]{2,1,0:T(8,128)S(1)}, f32[4,256,256]{2,1,0:T(8,128)}, u32[]{:S(2)}) copy-start(f32[4,256,256]{2,1,0:T(8,128)} %gate_hbm.1) | copy-start | bytes 3145732
  1.9 1.0 %copy-start.1 = (f32[1,1,131072]{2,1,0:T(1,128)S(1)}, f32[1,1,131072]{2,1,0:T(1,128)}, u32[]{:S(2)}) copy-start(f32[1,1,131072]{2,1,0:T(1,128)} %param.5) | copy-start | bytes 1572868
  2.9 0.7 %copy-start.2 = (f32[4,2,2,256]{3,2,1,0:T(2,128)S(1)}, f32[4,2,2,256]{3,2,1,0:T(2,128)}, u32[]{:S(2)}) copy-start(f32[4,2,2,256]{3,2,1,0:T(2,128)} %closing_hbm.1) | copy-start | bytes 49156
  3.7 0.7 %copy-start.4 = (s32[2,8]{1,0:T(2,128)S(1)}, s32[2,8]{1,0:T(2,128)}, u32[]{:S(2)}) copy-start(s32[2,8]{1,0:T(2,128)} %orders_hbm.1) | copy-start | bytes 196

commit v2 on v1

--- a/solution.py
+++ b/solution.py
@@ -107,7 +107,18 @@
     return total
 
 
+def flipped(index, mask):
+    bit = 1
+    while bit <= mask:
+        if mask & bit:
+            index = index + bit - 2 * bit * (index // bit % 2)
+        bit *= 2
+    return index
+
+
 def kernel(
+    group,
+    order,
     count_hi,
     count_lo,
     x_hbm,
@@ -126,6 +137,7 @@
     edges_far,
     first_ref,
     second_ref,
+    sums,
     part_near,
     part_far,
     result,
@@ -145,7 +157,7 @@
     turns = edges_ref.shape[0]
     edges = gate_ref.shape[0]
     offsets = [
-        (a, b) for a in range(count_hi - 1, -1, -1) for b in range(count_lo) if a or b
+        (a, b) for a in range(count_hi) for b in range(count_lo) if a or b
     ]
     pairs = (
         (x_hbm, x_ref),
@@ -159,7 +171,7 @@
         get.start()
 
     def target(a, b):
-        return lax.rem(hi + a, count_hi), lax.rem(lo + b, count_lo)
+        return flipped(hi, a), flipped(lo, b)
 
     barrier = pltpu.get_barrier_semaphore()
     for a, b in offsets:
@@ -189,8 +201,9 @@
             device_id={"hi": th, "lo": tl},
             device_id_type=MESH,
         )
-        copy.start()
         sends.append(copy)
+    for k in [0] + list(range(len(offsets) - 1, 0, -1)):
+        sends[k].start()
     gets[1].wait()
     edge_copy = pltpu.make_async_remote_copy(
         src_ref=edges_ref,
@@ -206,6 +219,7 @@
     down = lax.broadcasted_iota(jnp.int32, (GATE, GATE), 0)
     along = lax.broadcasted_iota(jnp.int32, (GATE, GATE), 1)
     per = span_hi // 2
+    wide = group * span_hi
     column = (down // rows * per + down % per) * count_hi + down % rows // per
     columns = (column == along).astype(FULL).astype(HALF)
     rows_one = source_row(along % span_hi * count_hi + along // span_hi, orders_ref, 0)
@@ -233,31 +247,43 @@
             moved = dot(columns, piece, ((1,), (1,))).astype(HALF)
             moved = dot(moved, rows_one).astype(HALF)
             for side in range(2):
-                first_ref[part, side, pl.ds(s * rows, rows), :] = moved[
-                    side * rows : (side + 1) * rows
-                ]
+                for c in range(count_hi // group):
+                    first_ref[part, c, side, :, s * wide : (s + 1) * wide] = moved[
+                        side * rows : (side + 1) * rows, c * wide : (c + 1) * wide
+                    ]
         for part, piece in enumerate(halves(pick(1, lambda c: gate_ref[c]) * rear)):
-            second_ref[part, pl.ds(s * GATE, GATE), :] = dot(rows_two, piece).astype(HALF)
-
-    for copy in sends:
-        copy.wait_recv()
-    x_high, x_low = halves(jnp.concatenate([arrived[i] for i in range(count_lo)], axis=1))
-
-    def amplitudes(side):
-        high, low = first_ref[0, side], first_ref[1, side]
-        inner = dot(high, x_high) + dot(high, x_low) + dot(low, x_high)
-        inner_high, inner_low = halves(inner)
-        total = None
+            second_ref[part, s] = dot(rows_two, piece).astype(HALF)
+
+    def advance(step):
+        for copy, (a, b) in zip(sends, offsets):
+            if a // group == step:
+                copy.wait_recv()
+        c = flipped(hi // group, step)
+        place = pl.ds(pl.multiple_of(c * wide, wide), wide)
+        piece = jnp.concatenate([arrived[i, place, :] for i in range(count_lo)], axis=1)
+        high, low = halves(piece)
+        inner = []
         for s in range(2 * turns):
-            left_high = inner_high[s * rows : (s + 1) * rows]
-            left_low = inner_low[s * rows : (s + 1) * rows]
-            right_high = second_ref[0, pl.ds(s * GATE, GATE), :]
-            right_low = second_ref[1, pl.ds(s * GATE, GATE), :]
-            term = dot(left_high, right_high) + dot(left_high, right_low) + dot(left_low, right_high)
-            total = term if total is None else total + term
-        return total
-
-    part_near[...] = amplitudes(other)
+            inner.append(
+                dot(high, second_ref[0, s]) + dot(low, second_ref[0, s]) + dot(high, second_ref[1, s])
+            )
+        high, low = halves(jnp.concatenate(inner, axis=0))
+
+        def side_sum(side):
+            left, rest = first_ref[0, c, side], first_ref[1, c, side]
+            return dot(left, high) + dot(left, low) + dot(rest, high)
+
+        return side_sum
+
+    for i, step in enumerate(order[:-1]):
+        side_sum = advance(step)
+        for side in range(2):
+            if i == 0:
+                sums[side] = side_sum(side)
+            else:
+                sums[side] += side_sum(side)
+    side_sum = advance(order[-1])
+    part_near[...] = sums[other] + side_sum(other)
     part_copy = pltpu.make_async_remote_copy(
         src_ref=part_near,
         dst_ref=part_far,
@@ -267,7 +293,7 @@
         device_id_type=MESH,
     )
     part_copy.start()
-    own = amplitudes(cut)
+    own = sums[cut] + side_sum(cut)
     part_copy.wait_recv()
     own = own + part_far[...]
     for b in range(count_hi):
@@ -309,12 +335,14 @@
     fits = middle == 1 and span_lo == 128 and span_hi % 16 == 0
     if not fits or lax.axis_size("cuts") != CLOSED:
         return local_plain(state_block, gate_table, closing_table, slice_edges, bit_orders)
+    group = 1
+    order = (0, 1, 3, 2) if count_hi == 4 else tuple(range(count_hi // group))
     slices = slice_edges.shape[0] * CLOSED
     rows = GATE // 2
     hbm = pl.BlockSpec(memory_space=pltpu.HBM)
     dma = pltpu.SemaphoreType.DMA
     out = pl.pallas_call(
-        functools.partial(kernel, count_hi, count_lo),
+        functools.partial(kernel, group, order, count_hi, count_lo),
         out_shape=jax.ShapeDtypeStruct((span_hi // 2 * blocks, span_lo), FULL),
         in_specs=[hbm] * 5,
         out_specs=pl.BlockSpec(memory_space=pltpu.VMEM),
@@ -327,8 +355,9 @@
             pltpu.VMEM((blocks, span_hi, span_lo), FULL),
             pltpu.VMEM((count_lo, GATE, span_lo), FULL),
             pltpu.VMEM(slice_edges.shape, jnp.int32),
-            pltpu.VMEM((2, 2, slices * rows, GATE), HALF),
-            pltpu.VMEM((2, slices * GATE, GATE), HALF),
+            pltpu.VMEM((2, count_hi // group, 2, rows, slices * group * span_hi), HALF),
+            pltpu.VMEM((2, slices, GATE, GATE), HALF),
+            pltpu.VMEM((2, rows, GATE), FULL),
             pltpu.VMEM((rows, GATE), FULL),
             pltpu.VMEM((rows, GATE), FULL),
             pltpu.VMEM((blocks, span_hi // 2, span_lo), FULL),
@@ -342,7 +371,7 @@
             dma((blocks,)),
         ],
         compiler_params=pltpu.CompilerParams(
-            collective_id=0, has_side_effects=True, vmem_limit_bytes=32 * 1024 * 1024
+            collective_id=0, has_side_effects=True, vmem_limit_bytes=67_043_328
         ),
     )(
         state_block.reshape(-1, span_lo),

time: 26.8 us -> 22.3 us (0.83)
  local copies, waits for them, and re-layouts: 5 us -> 1.57 us
  Pallas kernels: 21.5 us -> 20.6 us
    unnamed x11 -> x1, local copies, waits for them, and re-layouts: 5 us -> 1.57 us
    pallas_call x1, Pallas kernels: 21.5 us -> 20.6 us  [local(): pl.pallas_call(functools.partial(kernel, group, order, count_hi, count_lo...]
where the time goes in v2:
time: 22.3 us; the launch traced here: 22.2 us
  Pallas kernels  20.6 us (92%)
  local copies, waits for them, and re-layouts  1.57 us (7%)
    pallas_call x1, Pallas kernels, local(): pl.pallas_call(functools.partial(kernel, group, order, count_hi, count_lo...  20.6 us
    unnamed x1, local copies, waits for them, and re-layouts  1.57 us

profile of v2, /device:TPU:0, one launch (start us, length us, event | category | flops | bytes accessed | tf_op | source)
XLA Modules:
  0.0 22.2 jit_solution(36179448339905689)
XLA Ops:
  0.0 20.6 %shard_map.55 = f32[256,128]{1,0:T(8,128)} custom-call(f32[1024,128]{1,0:T(8,128)} %bitcast.2, f32[4,256,256]{2,1,0:T(8,128)} %gate_hbm.1, f32[4,2,2,256]{3,2,1,0:T(2,128)} %closing_hbm.1, s32[2,3]{1,0:T(2,128)} %edges_hbm.1, s32[2,8]{1,0:T(2,128)} %orders_hbm.1), custom_call_target="tpu_custom_call" | custom-call | tf_op jit(solution)/shard_map/pallas_call | solution.py:344
  20.6 1.6 %copy.7 = f32[1,1,32768]{2,1,0:T(1,128)} copy(f32[1,1,32768]{2,1,0:T(1,128)} %bitcast.3) | data formatting | bytes 262144

commit v3 on v2

--- a/solution.py
+++ b/solution.py
@@ -311,13 +311,16 @@
             device_id={"hi": th, "lo": tl},
             device_id_type=MESH,
         )
-        copy.start()
         outs.append(copy)
-    landed[here] = result[here]
-    for copy in outs:
+    for k in range(len(offsets) - 1, -1, -1):
+        outs[k].start()
+    blocks = count_hi * count_lo
+    out_ref[pl.ds(here, per, stride=blocks), :] = result[here]
+    for copy, (a, b) in zip(outs, offsets):
         copy.wait_recv()
-    for j in range(count_hi * count_lo):
-        out_ref[pl.ds(j, per, stride=count_hi * count_lo), :] = landed[j]
+        th, tl = target(a, b)
+        j = th * count_lo + tl
+        out_ref[pl.ds(j, per, stride=blocks), :] = landed[j]
     for copy in sends:
         copy.wait_send()
     part_copy.wait_send()
@@ -371,14 +374,19 @@
             dma((blocks,)),
         ],
         compiler_params=pltpu.CompilerParams(
-            collective_id=0, has_side_effects=True, vmem_limit_bytes=67_043_328
+            collective_id=0, has_side_effects=True, vmem_limit_bytes=32 * 1024 * 1024
         ),
     )(
-        state_block.reshape(-1, span_lo),
-        gate_table,
-        closing_table,
-        slice_edges,
-        bit_orders,
+        *(
+            pltpu.with_memory_space_constraint(item, pltpu.HBM)
+            for item in (
+                state_block.reshape(-1, span_lo),
+                gate_table,
+                closing_table,
+                slice_edges,
+                bit_orders,
+            )
+        )
     )
     return out.reshape(1, 1, -1)
 

time: 22.3 us -> 19.8 us (0.89)
  the two profiles are of different devices: /device:TPU:0 before, /device:TPU:1 now
where the time goes in v3:
time: 19.8 us; the launch traced here: 19.7 us
  Pallas kernels  19 us (96%)
  local copies, waits for them, and re-layouts  0.66 us (3%)
    pallas_call x1, Pallas kernels, local(): pl.pallas_call(functools.partial(kernel, group, order, count_hi, count_lo...  19 us
    unnamed x1, local copies, waits for them, and re-layouts  0.66 us

profile of v3, /device:TPU:1, one launch (start us, length us, event | category | flops | bytes accessed | tf_op | source)
XLA Modules:
  0.0 19.7 jit_solution(10710615069611445440)
XLA Ops:
  0.0 19.0 %shard_map.55 = f32[256,128]{1,0:T(8,128)S(1)} custom-call(f32[1024,128]{1,0:T(8,128)} %bitcast.3, f32[4,256,256]{2,1,0:T(8,128)} %gate_hbm.1, f32[4,2,2,256]{3,2,1,0:T(2,128)} %closing_hbm.1, s32[2,3]{1,0:T(2,128)} %edges_hbm.1, s32[2,8]{1,0:T(2,128)} %orders_hbm.1), custom_call_target="tpu_custom_call" | custom-call | tf_op jit(solution)/shard_map/pallas_call | solution.py:347
  19.0 0.7 %copy.7 = f32[1,1,32768]{2,1,0:T(1,128)} copy(f32[1,1,32768]{2,1,0:T(1,128)S(1)} %bitcast.2) | data formatting | bytes 262144
